TPU v7x, 32 devices: a whole 2x2x4 slice. The times are simulated.
32 devices in a mesh: gx: 4 (over y, x), gy: 4 (over z), gz: 2 (over core).
Axes of the slice: x: 2, y: 2, z: 4, core: 2. Of those that a mesh axis runs over, the one named last changes fastest.
Arguments:
- start: float32 [4, 4, 2, 1, 32, 1024], P('gx', 'gy', 'gz'), may hold values from -6 to 6
- stencils: float32 [6, 4, 4, 2, 32, 32], P(None, 'gx', 'gy', 'gz'), as said below
Outputs:
- basis: float32 [4, 4, 2, 1, 5, 32, 1024], P('gx', 'gy', 'gz')
- coefficients: float32 [1, 2, 5], replicated
Inputs may be any that keep to these rules, and one draw needn't show every extreme that they name: `stencils`: each of a patch's six matrices is symmetric positive definite.
All inputs are finite; a program needn't handle non-finite values.
Results may differ from a plain program's by a relative error of at most 0.0003.
Values sent between devices are 32-bit elements; how exact they have to be, the bound alone decides.
A program may use at most 128 MiB of HBM per device.

v0:
```python
import jax
import jax.numpy as jnp
from jax import lax
from jax.sharding import PartitionSpec as P

ITERS = 5


def padded_2(block, sides, width):
    for axis, dim in sides:
        count = lax.axis_size(axis)
        forward = [(i, i + 1) for i in range(count - 1)]
        backward = [(target, source) for source, target in forward]
        low = lax.ppermute(
            lax.slice_in_dim(block, block.shape[dim] - width, None, axis=dim), axis, forward
        )
        high = lax.ppermute(lax.slice_in_dim(block, 0, width, axis=dim), axis, backward)
        block = jnp.concatenate([low, block, high], axis=dim)
    return block


def along(field, matrix, dim):
    forms = ["pabc,ea->pebc", "pabc,eb->paec", "pabc,ec->pabe"]
    return jnp.einsum(forms[dim - 1], field, matrix, precision=lax.Precision.HIGHEST)


def fold_padded(padded, dim):
    length = padded.shape[dim]
    core = lax.slice_in_dim(padded, 1, length - 1, 1, dim)
    inner = core.shape[dim]
    lower = lax.slice_in_dim(padded, 0, 1, 1, dim)
    upper = lax.slice_in_dim(padded, length - 1, length, 1, dim)
    first = lax.slice_in_dim(core, 0, 1, 1, dim) + lower
    last = lax.slice_in_dim(core, inner - 1, inner, 1, dim) + upper
    middle = lax.slice_in_dim(core, 1, inner - 1, 1, dim)
    return jnp.concatenate([first, middle, last], axis=dim)


def assemble(field):
    padded = padded_2(field, (("gx", 1), ("gy", 2), ("gz", 3)), 1)
    padded = fold_padded(padded, 1)
    padded = fold_padded(padded, 2)
    return fold_padded(padded, 3)


def weight_along(index, groups, count):
    plane = jnp.arange(count)
    shared = (plane == 0) & (index > 0) | (plane == count - 1) & (index < groups - 1)
    return jnp.where(shared, 0.5, 1.0).astype(jnp.float32)


def operate(field, mats):
    first = along(field, mats[5], 3)
    second = along(first, mats[4], 2)
    term_one = along(second, mats[0], 1)
    third = along(first, mats[1], 2)
    fourth = along(field, mats[2], 3)
    fifth = along(fourth, mats[4], 2)
    term_two = along(third + fifth, mats[3], 1)
    return assemble(term_one + term_two)


def local_dot(weights, left, right):
    return jnp.sum(weights[None] * left * right, axis=(1, 2, 3))


def shards(start, stencils):
    probes = start.shape[3]
    count = start.shape[4]
    start = start.reshape(probes, count, count, count)
    mats = stencils.reshape(6, count, count)
    weight_x = weight_along(lax.axis_index("gx"), lax.axis_size("gx"), count)
    weight_y = weight_along(lax.axis_index("gy"), lax.axis_size("gy"), count)
    weight_z = weight_along(lax.axis_index("gz"), lax.axis_size("gz"), count)
    weights = weight_x[:, None, None] * weight_y[None, :, None] * weight_z[None, None, :]
    first = assemble(weights[None] * start)
    squared = lax.psum(local_dot(weights, first, first), ("gx", "gy", "gz"))
    vector = first / jnp.sqrt(squared)[:, None, None, None]
    vectors = [vector]
    alphas = []
    betas = []
    for j in range(ITERS):
        image = operate(vectors[j], mats)
        stacked = jnp.stack(vectors)
        heights, length = lax.psum(
            (
                jnp.sum(weights[None, None] * stacked * image[None], axis=(2, 3, 4)),
                local_dot(weights, image, image),
            ),
            ("gx", "gy", "gz"),
        )
        alpha = heights[j]
        for i in range(j + 1):
            image = image - heights[i][:, None, None, None] * vectors[i]
        beta = jnp.sqrt(length - jnp.sum(heights * heights, axis=0))
        vectors.append(image / beta[:, None, None, None])
        alphas.append(alpha)
        betas.append(beta)
    coefficients = jnp.stack([jnp.stack(alphas, axis=1), jnp.stack(betas, axis=1)], axis=1)
    basis = jnp.stack(vectors[1:], axis=1)
    return (basis.reshape(1, 1, 1, probes, ITERS, count, count * count), coefficients)


def solution(mesh):
    return jax.shard_map(
        shards,
        mesh=mesh,
        in_specs=(P("gx", "gy", "gz", None, None, None), P(None, "gx", "gy", "gz", None, None)),
        out_specs=(P("gx", "gy", "gz", None, None, None, None), P()),
        check_vma=False,
    )
```

profile of v0, /device:TPU:0, one launch (start us, length us, event | category | flops | bytes accessed | tf_op | source)
XLA Modules:
  0.0 597.5 jit_solution(12451091613436732356)
XLA Ops:
  2.0 4.9 collective-permute-start
  8.4 4.2 collective-permute-done.1
  12.6 3.5 collective-permute-start.2
  17.5 4.2 collective-permute-done.3
  31.1 40.2 %psum.77 = f32[1]{0:T(128)} all-reduce(f32[1]{0:T(128)} %bitcast.3), channel_id=1, replica_groups=mesh['gx'=4,'gy'=4,'gz'=2] {'gx','gy','gz'}, use_global_device_ids=true, to_apply=%region_1.2 | all-reduce | flops 1 | bytes 8 | tf_op jit(solution)/shard_map/psum | solution.py:77
  72.4 2.5 fusion.90
  74.9 2.5 fusion.60
  85.4 4.2 collective-permute-start.6
  91.0 4.2 collective-permute-done.7
  98.9 4.1 collective-permute-done.9
  119.7 41.5 %all-reduce.4 = (f32[1]{0:T(128)}, f32[1,1]{1,0:T(1,128)}) all-reduce(f32[1]{0:T(128)} %bitcast.37, f32[1,1]{1,0:T(1,128)} %bitcast.32), channel_id=1, replica_groups=mesh['gx'=4,'gy'=4,'gz'=2] {'gx','gy','gz'}, use_global_device_ids=true, to_apply=%region_5.6 | all-reduce | flops 2 | bytes 16 | tf_op jit(solution)/shard_map/psum | solution.py:85
  163.2 2.7 fusion.26
  165.9 2.5 fusion.88
  168.4 2.5 fusion.58
  182.6 4.2 collective-permute-start.12
  188.2 4.2 collective-permute-done.13
  197.3 2.9 collective-permute-done.15
  217.5 41.5 %all-reduce.3 = (f32[1]{0:T(128)}, f32[2,1]{0,1:T(1,128)S(1)}) all-reduce(f32[1]{0:T(128)} %bitcast.68, f32[2,1]{0,1:T(1,128)S(1)} %bitcast.384), channel_id=1, replica_groups=mesh['gx'=4,'gy'=4,'gz'=2] {'gx','gy','gz'}, use_global_device_ids=true, to_apply=%region_9.10 | all-reduce | flops 3 | bytes 24 | tf_op jit(solution)/shard_map/psum | solution.py:85
  261.6 3.3 fusion.28
  265.0 2.5 fusion.86
  267.4 2.5 fusion.56
  273.7 2.5 fusion.46
  279.9 4.2 collective-permute-start.18
  285.5 4.2 collective-permute-done.19
  294.9 2.6 collective-permute-done.21
  304.4 4.3 constant_dynamic-update-slice_fusion.1
  318.1 41.4 %all-reduce.2 = (f32[1]{0:T(128)}, f32[3,1]{0,1:T(1,128)S(1)}) all-reduce(f32[1]{0:T(128)} %bitcast.94, f32[3,1]{0,1:T(1,128)S(1)} %bitcast.386), channel_id=1, replica_groups=mesh['gx'=4,'gy'=4,'gz'=2] {'gx','gy','gz'}, use_global_device_ids=true, to_apply=%region_14.15 | all-reduce | flops 4 | bytes 32 | tf_op jit(solution)/shard_map/psum | solution.py:85
  362.1 3.9 fusion.31
  366.0 2.5 fusion.84
  368.5 2.5 fusion.54
  380.8 4.2 collective-permute-start.24
  386.5 4.1 collective-permute-done.25
  394.1 4.2 collective-permute-done.27
  405.2 4.9 constant_dynamic-update-slice_fusion
  419.5 41.5 %all-reduce.1 = (f32[1]{0:T(128)}, f32[4,1]{0,1:T(1,128)S(1)}) all-reduce(f32[1]{0:T(128)} %bitcast.121, f32[4,1]{0,1:T(1,128)S(1)} %bitcast.385), channel_id=1, replica_groups=mesh['gx'=4,'gy'=4,'gz'=2] {'gx','gy','gz'}, use_global_device_ids=true, to_apply=%region_19.20 | all-reduce | flops 5 | bytes 40 | tf_op jit(solution)/shard_map/psum | solution.py:85
  463.7 4.7 fusion.35
  468.4 2.5 fusion.82
  470.9 2.5 fusion.52
  481.4 4.2 collective-permute-start.30
  487.0 4.2 collective-permute-done.31
  494.6 4.3 collective-permute-done.33
  506.1 7.2 %bitcast_dynamic-update-slice_fusion = f32[5,1,32,32,32]{4,3,2,1,0:T(8,128)} fusion(f32[5,1,32,32,32]{4,3,2,1,0:T(8,128)} %get-tuple-element.16, f32[1,32,32,32]{3,2,1,0:T(8,128)S(1)} %copy-done.6, f32[1,32,32,32]{3,2,1,0:T(8,128)} %copy-done.41, f32[1,32,32,32]{3,2,1,0:T(8,128)S(1)} %get-tuple-element.21, f32[]{:T(128)} %bitcast.123, f32[]{:T(128)} %bitcast.120, ...), kind=kLoop, calls=%fused_computation.111 | loop fusion | flops 622592 | bytes 1971712 | tf_op jit(solution)/shard_map/stack | solution.py:84
  519.3 41.7 %all-reduce = (f32[5,1]{0,1:T(1,128)S(1)}, f32[1]{0:T(128)}) all-reduce(f32[5,1]{0,1:T(1,128)S(1)} %bitcast.387, f32[1]{0:T(128)} %bitcast.149), channel_id=1, replica_groups=mesh['gx'=4,'gy'=4,'gz'=2] {'gx','gy','gz'}, use_global_device_ids=true, to_apply=%region_22.23 | all-reduce | flops 6 | bytes 48 | tf_op jit(solution)/shard_map/psum | solution.py:85
  563.5 3.6 maximum_subtract_fusion.8
  567.2 6.5 %maximum_subtract_fusion.6 = (f32[1,1,32,32,32]{4,3,2,1,0:T(8,128)}, f32[1,1,32,32,32]{4,3,2,1,0:T(8,128)}, f32[1,1,32,32,32]{4,3,2,1,0:T(8,128)}, f32[1,1,32,32,32]{4,3,2,1,0:T(8,128)}) fusion(f32[1,1,32,32,1]{4,3,2,1,0:T(8,128)S(1)} %bitcast.377, f32[1,1,32,32,30]{4,3,2,1,0:T(8,128)} %get-tuple-element.71, f32[1,1,32,32,1]{4,3,2,1,0:T(8,128)S(1)} %bitcast.375, ...), kind=kLoop, calls=%fused_computation.101 | loop fusion | flops 557056 | bytes 1179668 | tf_op jit(solution)/shard_map/sub | solution.py:94
  579.1 3.3 stack.85
  585.8 3.8 constant_dynamic-update-slice_fusion.4
  589.6 6.5 %divide_dynamic-update-slice_fusion = f32[1,1,1,1,5,32,1024]{6,5,4,3,2,1,0:T(8,128)S(1)} fusion(f32[1,1,1,1,5,32,1024]{6,5,4,3,2,1,0:T(8,128)S(1)} %constant_dynamic-update-slice_fusion.4, f32[1,1,1,1,1,32,1024]{6,5,4,3,2,1,0:T(8,128)S(1)} %sub.751, f32[1,1,1,1,1,32,1024]{6,5,4,3,2,1,0:T(8,128)S(1)} %div.537, f32[]{:T(128)} %bitcast.151, f32[]{:T(128)} %bitcast.148, ...), kind=kLoop, calls=%fused_computation.127 | loop fusion | flops 786432 | bytes 786488 | tf_op jit(solution)/shard_map/stack | solution.py:100
  (336 shorter events, 180.3 us)
Async XLA Ops:
  2.0 6.3 %collective-permute-start = (f32[1,1,32,32]{3,2,1,0:T(8,128)S(1)}, f32[1,1,32,32]{3,2,1,0:T(8,128)S(1)}, u32[]{:S(2)}, u32[]{:S(2)}) collective-permute-start(f32[1,1,32,32]{3,2,1,0:T(8,128)S(1)} %get-tuple-element.110), channel_id=1, source_target_pairs={{0,8},{8,16},{16,24},{1,9},{9,17},{17,25},{2,10},{10,18},{18,26},{... | collective-permute-start | bytes 12296 | tf_op jit(solution)/shard_map/ppermute | solution.py:14
  6.9 5.6 collective-permute-start.1
  12.6 4.9 collective-permute-start.2
  16.1 5.6 collective-permute-start.3
  22.4 2.9 collective-permute-start.4
  24.0 3.1 collective-permute-start.5
  30.0 42.3 %copy-start.45 = (f32[6,1,1,1,32,32]{5,4,3,2,1,0:T(8,128)S(1)}, f32[6,1,1,1,32,32]{5,4,3,2,1,0:T(8,128)}, u32[]{:S(2)}) copy-start(f32[6,1,1,1,32,32]{5,4,3,2,1,0:T(8,128)} %param.3) | copy-start | bytes 73732
  85.4 5.6 collective-permute-start.6
  89.6 5.6 collective-permute-start.7
  95.3 3.6 collective-permute-start.8
  97.4 5.6 collective-permute-start.9
  105.9 5.2 collective-permute-start.10
  108.6 3.2 collective-permute-start.11
  117.7 45.5 %copy-start.24 = (f32[1,32,32,1]{3,2,1,0:T(8,128)}, f32[1,32,32,1]{3,2,1,0:T(8,128)S(1)}, u32[]{:S(2)}) copy-start(f32[1,32,32,1]{3,2,1,0:T(8,128)S(1)} %get-tuple-element.104) | copy-start | bytes 12292
  165.9 8.3 %copy-start = (f32[32,32,32]{2,1,0:T(8,128)}, f32[32,32,32]{2,1,0:T(8,128)S(1)}, u32[]{:S(2)}) copy-start(f32[32,32,32]{2,1,0:T(8,128)S(1)} %fusion.26) | copy-start | bytes 393220
  182.6 5.6 collective-permute-start.12
  186.8 5.6 collective-permute-start.13
  192.4 4.8 collective-permute-start.14
  194.6 5.6 collective-permute-start.15
  203.1 5.6 collective-permute-start.16
  205.8 4.2 collective-permute-start.17
  215.6 46.0 %copy-start.1 = (f32[32,32,32]{2,1,0:T(8,128)S(1)}, f32[32,32,32]{2,1,0:T(8,128)}, u32[]{:S(2)}) copy-start(f32[32,32,32]{2,1,0:T(8,128)} %copy-done) | copy-start | bytes 393220
  279.9 5.6 collective-permute-start.18
  284.1 5.6 collective-permute-start.19
  289.7 5.1 collective-permute-start.20
  291.8 5.6 collective-permute-start.21
  300.4 8.3 %collective-permute-start.22 = (f32[1,34,34,1]{2,3,1,0:T(1,128)S(1)}, f32[1,34,34,1]{2,3,1,0:T(1,128)S(1)}, u32[]{:S(2)}, u32[]{:S(2)}) collective-permute-start(f32[1,34,34,1]{2,3,1,0:T(1,128)S(1)} %copy.397), channel_id=1, source_target_pairs={{0,1},{2,3},{4,5},{6,7},{8,9},{10,11},{12,13},{14,15},{16,17},{18,... | collective-permute-start | bytes 13880 | tf_op jit(solution)/shard_map/ppermute | solution.py:14
  303.1 6.8 %collective-permute-start.23 = (f32[1,34,34,1]{2,3,1,0:T(1,128)S(1)}, f32[1,34,34,1]{2,3,1,0:T(1,128)S(1)}, u32[]{:S(2)}, u32[]{:S(2)}) collective-permute-start(f32[1,34,34,1]{2,3,1,0:T(1,128)S(1)} %copy.398), channel_id=1, source_target_pairs={{1,0},{3,2},{5,4},{7,6},{9,8},{11,10},{13,12},{15,14},{17,16},{19,... | collective-permute-start | bytes 13880 | tf_op jit(solution)/shard_map/ppermute | solution.py:17
  315.4 46.7 %copy-start.2 = (f32[32,32,32]{2,1,0:T(8,128)S(1)}, f32[32,32,32]{2,1,0:T(8,128)}, u32[]{:S(2)}) copy-start(f32[32,32,32]{2,1,0:T(8,128)} %copy-done) | copy-start | bytes 393220
  380.8 5.7 collective-permute-start.24
  385.0 5.6 collective-permute-start.25
  390.7 3.4 collective-permute-start.26
  392.7 5.6 collective-permute-start.27
  401.2 8.9 %collective-permute-start.28 = (f32[1,34,34,1]{2,3,1,0:T(1,128)S(1)}, f32[1,34,34,1]{2,3,1,0:T(1,128)S(1)}, u32[]{:S(2)}, u32[]{:S(2)}) collective-permute-start(f32[1,34,34,1]{2,3,1,0:T(1,128)S(1)} %copy.412), channel_id=1, source_target_pairs={{0,1},{2,3},{4,5},{6,7},{8,9},{10,11},{12,13},{14,15},{16,17},{18,... | collective-permute-start | bytes 13880 | tf_op jit(solution)/shard_map/ppermute | solution.py:14
  403.9 7.4 %collective-permute-start.29 = (f32[1,34,34,1]{2,3,1,0:T(1,128)S(1)}, f32[1,34,34,1]{2,3,1,0:T(1,128)S(1)}, u32[]{:S(2)}, u32[]{:S(2)}) collective-permute-start(f32[1,34,34,1]{2,3,1,0:T(1,128)S(1)} %copy.413), channel_id=1, source_target_pairs={{1,0},{3,2},{5,4},{7,6},{9,8},{11,10},{13,12},{15,14},{17,16},{19,... | collective-permute-start | bytes 13880 | tf_op jit(solution)/shard_map/ppermute | solution.py:17
  417.6 46.1 %copy-start.3 = (f32[32,32,32]{2,1,0:T(8,128)S(1)}, f32[32,32,32]{2,1,0:T(8,128)}, u32[]{:S(2)}) copy-start(f32[32,32,32]{2,1,0:T(8,128)} %copy-done) | copy-start | bytes 393220
  481.4 5.6 collective-permute-start.30
  485.6 5.6 collective-permute-start.31
  491.2 3.4 collective-permute-start.32
  493.2 12.9 %copy-start.6 = (f32[1,32,32,32]{3,2,1,0:T(8,128)S(1)}, f32[1,32,32,32]{3,2,1,0:T(8,128)}, u32[]{:S(2)}) copy-start(f32[1,32,32,32]{3,2,1,0:T(8,128)} %get-tuple-element.19) | copy-start | bytes 393220
  493.2 5.8 collective-permute-start.33
  501.8 11.5 %collective-permute-start.34 = (f32[1,34,34,1]{2,3,1,0:T(1,128)S(1)}, f32[1,34,34,1]{2,3,1,0:T(1,128)S(1)}, u32[]{:S(2)}, u32[]{:S(2)}) collective-permute-start(f32[1,34,34,1]{2,3,1,0:T(1,128)S(1)} %copy.427), channel_id=1, source_target_pairs={{0,1},{2,3},{4,5},{6,7},{8,9},{10,11},{12,13},{14,15},{16,17},{18,... | collective-permute-start | bytes 13880 | tf_op jit(solution)/shard_map/ppermute | solution.py:14
  504.5 9.2 %collective-permute-start.35 = (f32[1,34,34,1]{2,3,1,0:T(1,128)S(1)}, f32[1,34,34,1]{2,3,1,0:T(1,128)S(1)}, u32[]{:S(2)}, u32[]{:S(2)}) collective-permute-start(f32[1,34,34,1]{2,3,1,0:T(1,128)S(1)} %copy.428), channel_id=1, source_target_pairs={{1,0},{3,2},{5,4},{7,6},{9,8},{11,10},{13,12},{15,14},{17,16},{19,... | collective-permute-start | bytes 13880 | tf_op jit(solution)/shard_map/ppermute | solution.py:17
  519.3 47.9 %copy-start.20 = (f32[1,32,32,1]{3,2,1,0:T(8,128)S(1)}, f32[1,32,32,1]{3,2,1,0:T(8,128)}, u32[]{:S(2)}) copy-start(f32[1,32,32,1]{3,2,1,0:T(8,128)} %copy-done.19) | copy-start | bytes 12292
  519.3 47.9 %copy-start.22 = (f32[1,32,32,1]{3,2,1,0:T(8,128)S(1)}, f32[1,32,32,1]{3,2,1,0:T(8,128)}, u32[]{:S(2)}) copy-start(f32[1,32,32,1]{3,2,1,0:T(8,128)} %copy-done.21) | copy-start | bytes 12292
  519.3 47.9 %copy-start.25 = (f32[1,32,32,1]{3,2,1,0:T(8,128)S(1)}, f32[1,32,32,1]{3,2,1,0:T(8,128)}, u32[]{:S(2)}) copy-start(f32[1,32,32,1]{3,2,1,0:T(8,128)} %copy-done.24) | copy-start | bytes 12292
  519.3 47.9 %copy-start.27 = (f32[1,32,32,1]{3,2,1,0:T(8,128)S(1)}, f32[1,32,32,1]{3,2,1,0:T(8,128)}, u32[]{:S(2)}) copy-start(f32[1,32,32,1]{3,2,1,0:T(8,128)} %copy-done.26) | copy-start | bytes 12292
  561.0 6.2 %copy-start.39 = (f32[1,32,32,1]{3,2,1,0:T(8,128)S(1)}, f32[1,32,32,1]{3,2,1,0:T(8,128)}, u32[]{:S(2)}) copy-start(f32[1,32,32,1]{3,2,1,0:T(8,128)} %copy-done.38) | copy-start | bytes 12292
  (37 other events, 82.4 us)
where the time goes:
time: 609 us; the launch traced here: 597 us
  blocking collectives  248 us (41%)
  other arithmetic  92.7 us (15%)
  local copies, waits for them, and re-layouts  73 us (12%)
  starting transfers between devices  71.8 us (12%)
  matrix products  51.3 us (8%)
  waiting for transfers between devices  50.3 us (8%)
  between operations  10.5 us (2%)
    psum x5, blocking collectives, shards(): lax.psum((jnp.sum(weights[None, None] * stacked * image[None], axis=(2, 3...  208 us
    dot_general x35, matrix products, along(): jnp.einsum(forms[dim - 1], field, matrix, precision=lax.Precision.HIGHEST)  51.3 us
    ppermute x18, waiting for transfers between devices, padded_2(): lax.ppermute(lax.slice_in_dim(block, 0, width, axis=dim), axis, backward)  49.3 us
    ppermute x18, starting transfers between devices, padded_2(): lax.ppermute(lax.slice_in_dim(block, block.shape[dim] - width, None, axis...  47.2 us
    psum x1, blocking collectives, shards(): squared = lax.psum(local_dot(weights, first, first), ('gx', 'gy', 'gz'))  40.2 us
    ppermute x18, starting transfers between devices, padded_2(): lax.ppermute(lax.slice_in_dim(block, 0, width, axis=dim), axis, backward)  24.6 us
    unnamed x7, other arithmetic  18.4 us
    div x4, other arithmetic, shards(): vectors.append(image / beta[:, None, None, None])  14.6 us
  transfers between devices with their start and end apart: 36, of which 21 were waited for; matrix products, arithmetic and copies ran while one was open for 6% of the time, Pallas kernels for 0%

commit v1 on v0

v1 whole, which is shorter than its diff:
```python
import functools

import jax
import jax.numpy as jnp
from jax import lax
from jax.experimental import pallas as pl
from jax.experimental.pallas import tpu as pltpu
from jax.sharding import PartitionSpec as P

ITERS = 5
LANES = 128
SUB = 8
MESH = pl.DeviceIdType.MESH
F32 = jnp.float32
BF16 = jnp.bfloat16
HIGHEST = lax.Precision.HIGHEST


def iota(shape, dim):
    return lax.broadcasted_iota(jnp.int32, shape, dim)


def split(x):
    hi = x.astype(BF16)
    return hi, (x - hi.astype(F32)).astype(BF16)


def exact(a, b):
    return lax.dot_general(a, b, (((1,), (0,)), ((), ())), precision=HIGHEST, preferred_element_type=F32)


def mul(a, b):
    return jnp.dot(a, b, preferred_element_type=F32)


def swap(x):
    sub = iota((1, SUB, LANES), 1)
    group = iota((1, SUB, LANES), 2) >> 5
    s0, s1 = sub & 1, (sub >> 1) & 1
    g0, g1 = group & 1, (group >> 1) & 1
    far = pltpu.roll(x, 64, 2)
    x = jnp.where(s1 == g1, x, jnp.where(s1 == 0, pltpu.roll(far, SUB - 2, 1), pltpu.roll(far, 2, 1)))
    up = pltpu.roll(pltpu.roll(x, SUB - 1, 1), 32, 2)
    down = pltpu.roll(pltpu.roll(x, 1, 1), LANES - 32, 2)
    return jnp.where(s0 == g0, x, jnp.where(s0 == 0, up, down))


def build_matrices(st, mx, my, mz):
    count = st.shape[1]
    wide = LANES
    spread = ((iota((wide, count), 0) & (count - 1)) == iota((wide, count), 1)).astype(F32)
    spread_t = ((iota((count, wide), 1) & (count - 1)) == iota((count, wide), 0)).astype(F32)
    same = (iota((wide, wide), 0) >> 5) == (iota((wide, wide), 1) >> 5)
    for slot, which in ((0, 5), (1, 2)):
        big = exact(exact(spread, st[which].T), spread_t)
        hi, lo = split(jnp.where(same, big, 0.0))
        mz[0:wide, slot * wide:(slot + 1) * wide] = hi
        mz[wide:2 * wide, slot * wide:(slot + 1) * wide] = hi
        mz[2 * wide:3 * wide, slot * wide:(slot + 1) * wide] = lo
    rows = 2 * count
    r = iota((rows, count), 0)
    pick = (((r >> 3) * 4 + (r & 3)) == iota((rows, count), 1)).astype(F32)
    cols = 3 * rows
    l = iota((count, cols), 1) & (rows - 1)
    pick_t = (((l >> 3) * 4 + (l & 3)) == iota((count, cols), 0)).astype(F32)
    same = ((iota((rows, cols), 0) >> 2) & 1) == ((iota((rows, cols), 1) >> 2) & 1)
    middle = (iota((rows, cols), 1) >= rows) & (iota((rows, cols), 1) < 2 * rows)
    for slot, which in ((0, 4), (1, 1)):
        big = jnp.where(same, exact(exact(pick, st[which]), pick_t), 0.0)
        hi = big.astype(BF16).astype(F32)
        my[slot * rows:(slot + 1) * rows, :] = jnp.where(middle, big - hi, hi).astype(BF16)
    cols = 6 * count
    tile = ((iota((count, cols), 1) & (count - 1)) == iota((count, cols), 0)).astype(F32)
    stiff = exact(st[0], tile)
    mass = exact(st[3], tile)
    block = iota((count, cols), 1) >> 5
    big = jnp.where(block < 3, stiff, mass)
    hi = big.astype(BF16).astype(F32)
    mx[...] = jnp.where((block == 1) | (block == 4), big - hi, hi).astype(BF16)


def apply_patch(u, mx, my, mz):
    count, area = u.shape
    ni, nt = count // SUB, area // LANES
    tiles = jnp.concatenate(
        [u[SUB * i:SUB * (i + 1), LANES * t:LANES * (t + 1)] for i in range(ni) for t in range(nt)], axis=0
    )
    tiles = swap(tiles.reshape(ni * nt, SUB, LANES)).reshape(ni * nt * SUB, LANES)
    hi, lo = split(tiles)
    z = mul(jnp.concatenate([hi, lo, hi], axis=1), mz)
    rows = nt * SUB
    packed = []
    for slot in range(2):
        part = z[:, slot * LANES:(slot + 1) * LANES]
        wide = jnp.concatenate([part[rows * i:rows * (i + 1)] for i in range(ni)], axis=1)
        hi, lo = split(wide)
        packed.append(jnp.concatenate([hi, hi, lo], axis=0))
    both = mul(my, packed[0])
    first = both[:rows]
    second = both[rows:] + mul(my[:rows], packed[1])
    pieces = []
    for term in (first, second):
        stacked = jnp.concatenate([term[:, LANES * i:LANES * (i + 1)] for i in range(ni)], axis=0)
        stacked = swap(stacked.reshape(ni * nt, SUB, LANES))
        back = jnp.concatenate(
            [jnp.concatenate([stacked[i * nt + t] for i in range(ni)], axis=0) for t in range(nt)], axis=1
        )
        hi, lo = split(back)
        pieces += [hi, hi, lo]
    return mul(mx, jnp.concatenate(pieces, axis=0))


def kernel(sizes, start, st, basis, coef, mx, my, mz, wt, v0, field,
           zs, zr, xs, xr, ys, yr, es, er, rows, hsend, hrecv, rsend, rrecv):
    nx, ny, nz = sizes
    total = nx * ny * nz
    count, area = start.shape
    nt = area // LANES
    ni = count // SUB
    last = count - 1
    px, py, pz = lax.axis_index("gx"), lax.axis_index("gy"), lax.axis_index("gz")
    me = (px * ny + py) * nz + pz
    coords = (px, py, pz)
    there = [[coords[d] > 0, coords[d] < sizes[d] - 1] for d in range(3)]

    for ref in (zr, xr, yr, er):
        ref[...] = jnp.zeros_like(ref)
    barrier = pltpu.get_barrier_semaphore()

    def peer(k):
        p = lax.rem(me + k, total)
        return (p // (ny * nz), (p // nz) % ny, p % nz)

    def greet(k, carry):
        pl.semaphore_signal(barrier, inc=1, device_id=peer(k), device_id_type=MESH)
        return carry

    lax.fori_loop(1, total, greet, 0)

    def shared(index, d):
        return ((index == 0) & there[d][0]) | ((index == last) & there[d][1])

    lane = iota((count, area), 1)
    ia, ib, ic = iota((count, area), 0), lane >> 5, lane & (count - 1)
    half = lambda index, d: jnp.where(shared(index, d), 0.5, 1.0)
    weight = half(ia, 0) * half(ib, 1) * half(ic, 2)
    wt[...] = weight.astype(F32)
    field[...] = start[...] * wt[...]

    lane_c = iota((count, LANES), 1)
    face_c = (lane_c & (count - 1) == 0) | (lane_c & (count - 1) == last)
    even = (lane_c & 1) == 0
    lane8 = iota((SUB, LANES), 1)
    low8, high8 = lane8 < count, lane8 >= LANES - count
    lane1 = iota((1, LANES), 1)
    diag = iota((SUB, LANES), 0) == lane8

    def tile(t):
        return slice(t * LANES, (t + 1) * LANES)

    def remote(src, dst, phase, slot, target):
        return pltpu.make_async_remote_copy(
            src_ref=src, dst_ref=dst, send_sem=hsend.at[phase, slot], recv_sem=hrecv.at[phase, slot],
            device_id=target, device_id_type=MESH)

    def moved(dx, dy, dz):
        step = lambda d: 0 if d is None else 2 * d - 1
        return (px + step(dx), py + step(dy), pz + step(dz))

    def z_copies(phase):
        return [(remote(zs.at[phase], zr.at[phase, 1 - d], phase, 1 - d, moved(None, None, d)),
                 there[2][d]) for d in range(2)]

    def xy_copies(phase):
        out = []
        for d in range(2):
            out.append((remote(xs.at[phase, d], xr.at[phase, 1 - d], phase, 2 + 1 - d, moved(d, None, None)), there[0][d]))
            out.append((remote(ys.at[phase, d], yr.at[phase, 1 - d], phase, 4 + 1 - d, moved(None, d, None)), there[1][d]))
            for e in range(2):
                slot = 6 + 2 * (1 - d) + 1 - e
                out.append((remote(es.at[phase, 2 * d + e], er.at[phase, 2 * (1 - d) + 1 - e], phase, slot,
                                   moved(d, e, None)), there[0][d] & there[1][e]))
        return out

    def each(copies, act, flip):
        n = len(copies)
        for index, (copy, exists) in enumerate(copies):
            @pl.when(exists)
            def _():
                act(copy)

    def send_z(phase):
        packed = None
        for t in range(nt):
            part = jnp.where(face_c, field[:, tile(t)], 0.0)
            part = part if t == 0 else pltpu.roll(part, 2 * t, 1)
            packed = part if packed is None else packed + part
        zs[phase] = packed
        for copy, exists in z_copies(phase):
            @pl.when(exists)
            def _():
                copy.start()

    def wait_slot(ref, slot_sem):
        pltpu.make_async_copy(ref, ref, slot_sem).wait()

    def finish_halo(phase):
        for d in range(2):
            @pl.when(there[2][d])
            def _():
                wait_slot(zr.at[phase, d], hrecv.at[phase, d])
        merged = jnp.where(even, pltpu.roll(zr[phase, 0], LANES - last, 1), pltpu.roll(zr[phase, 1], last, 1))
        for t in range(nt):
            part = merged if t == 0 else pltpu.roll(merged, LANES - 2 * t, 1)
            field[:, tile(t)] += jnp.where(face_c, part, 0.0)
        for d in range(2):
            row = 0 if d == 0 else last
            for t in range(nt):
                xs[phase, d, t:t + 1, :] = field[row:row + 1, tile(t)]
            for e in range(2):
                es[phase, 2 * d + e] = field[row:row + 1, tile(0 if e == 0 else nt - 1)]
            packed = None
            for i in range(ni):
                block = field[SUB * i:SUB * (i + 1), tile(0 if d == 0 else nt - 1)]
                part = jnp.where(low8 if d == 0 else high8, block, 0.0)
                shift = (count * i + d * count) % LANES
                part = part if shift == 0 else pltpu.roll(part, shift, 1)
                packed = part if packed is None else packed + part
            ys[phase, d] = packed
        for copy, exists in xy_copies(phase):
            @pl.when(exists)
            def _():
                copy.start()

    def add_halo(phase):
        for d in range(2):
            @pl.when(there[0][d])
            def _():
                wait_slot(xr.at[phase, d], hrecv.at[phase, 2 + d])

            @pl.when(there[1][d])
            def _():
                wait_slot(yr.at[phase, d], hrecv.at[phase, 4 + d])
            for e in range(2):
                @pl.when(there[0][d] & there[1][e])
                def _():
                    wait_slot(er.at[phase, 2 * d + e], hrecv.at[phase, 6 + 2 * d + e])
        for d in range(2):
            received = yr[phase, d]
            for i in range(ni):
                shift = (-count * i - d * count) % LANES
                part = received if shift == 0 else pltpu.roll(received, shift, 1)
                field[SUB * i:SUB * (i + 1), tile(0 if d == 0 else nt - 1)] += jnp.where(low8 if d == 0 else high8, part, 0.0)
        for d in range(2):
            row = 0 if d == 0 else last
            for t in range(nt):
                line = xr[phase, d, t:t + 1, :]
                if t == 0:
                    line += jnp.where(lane1 < count, pltpu.roll(er[phase, 2 * d], count, 1), 0.0)
                if t == nt - 1:
                    line += jnp.where(lane1 >= LANES - count, pltpu.roll(er[phase, 2 * d + 1], LANES - count, 1), 0.0)
                field[row:row + 1, tile(t)] += line

    def send_dots(phase, products):
        packed = None
        for k, product in enumerate(products):
            acc = None
            for i in range(ni):
                for t in range(nt):
                    block = product[SUB * i:SUB * (i + 1), tile(t)]
                    acc = block if acc is None else acc + block
            line = jnp.where(iota((SUB, LANES), 0) == k, jnp.sum(acc, axis=0, keepdims=True), 0.0)
            packed = line if packed is None else packed + line
        sums = jnp.sum(packed, axis=1, keepdims=True)
        rows[phase, me] = jnp.sum(jnp.where(diag, sums, 0.0), axis=0, keepdims=True)

        def send(k, carry):
            pltpu.make_async_remote_copy(
                src_ref=rows.at[phase, me], dst_ref=rows.at[phase, me], send_sem=rsend.at[phase],
                recv_sem=rrecv.at[phase], device_id=peer(k), device_id_type=MESH).start()
            return carry

        lax.fori_loop(1, total, send, 0)

    def take_dots(phase):
        others = rows.at[phase, pl.ds(0, total - 1)]
        pltpu.make_async_copy(others, others, rrecv.at[phase]).wait()
        line = jnp.sum(rows[phase], axis=0)
        return jnp.sum(jnp.where(diag, line, 0.0), axis=1, keepdims=True)

    build_matrices(st, mx, my, mz)
    pl.semaphore_wait(barrier, total - 1)
    send_z(0)
    finish_halo(0)
    add_halo(0)
    vector = field[...]
    alpha = None
    row2, col2 = iota(coef.shape[1:], 0), iota(coef.shape[1:], 1)
    coefs = jnp.zeros(coef.shape[1:], F32)
    for j in range(ITERS):
        phase = j + 1
        image = apply_patch(vector, mx[...], my[...], mz[...])
        field[...] = image
        send_z(phase)
        old = [v0[...] if i == 0 else basis[i - 1] for i in range(j)]
        send_dots(phase, [wt[...] * vector * vector, image * vector] + [image * v for v in old])
        finish_halo(phase)
        add_halo(phase)
        sums = take_dots(phase)
        norm = jnp.sqrt(sums[0:1])
        inverse = 1.0 / norm
        if j > 0:
            coefs = jnp.where((row2 == 1) & (col2 == j - 1), norm * alpha, coefs)
        alpha = sums[1:2] / sums[0:1]
        coefs = jnp.where((row2 == 0) & (col2 == j), alpha, coefs)
        unit = vector * inverse
        if j == 0:
            v0[...] = unit
        else:
            basis[j - 1] = unit
        factor = inverse / alpha
        following = field[...] * factor - unit
        for i in range(j):
            following = following - (sums[2 + i:3 + i] * factor) * old[i]
        vector = following
    send_dots(ITERS + 1, [wt[...] * vector * vector])
    sums = take_dots(ITERS + 1)
    norm = jnp.sqrt(sums[0:1])
    coefs = jnp.where((row2 == 1) & (col2 == ITERS - 1), norm * alpha, coefs)
    basis[ITERS - 1] = vector * (1.0 / norm)
    coef[0] = coefs

    for phase in range(ITERS + 1):
        for copy, exists in z_copies(phase) + xy_copies(phase):
            @pl.when(exists)
            def _():
                copy.wait_send()
    for phase in range(1, ITERS + 2):
        others = rows.at[phase, pl.ds(0, total - 1)]
        pltpu.make_async_copy(others, others, rsend.at[phase]).wait()


def shards(sizes, start, stencils):
    probes, count, area = start.shape[3:]
    nt = area // LANES
    total = sizes[0] * sizes[1] * sizes[2]
    halos = ITERS + 1
    vmem = pl.BlockSpec(memory_space=pltpu.VMEM)
    call = pl.pallas_call(
        functools.partial(kernel, sizes),
        out_shape=(jax.ShapeDtypeStruct((ITERS, count, area), F32), jax.ShapeDtypeStruct((1, 2, ITERS), F32)),
        in_specs=[vmem, vmem],
        out_specs=(vmem, vmem),
        scratch_shapes=[
            pltpu.VMEM((count, 6 * count), BF16),
            pltpu.VMEM((4 * count, 6 * count), BF16),
            pltpu.VMEM((3 * LANES, 2 * LANES), BF16),
            pltpu.VMEM((count, area), F32),
            pltpu.VMEM((count, area), F32),
            pltpu.VMEM((count, area), F32),
            pltpu.VMEM((halos, count, LANES), F32),
            pltpu.VMEM((halos, 2, count, LANES), F32),
            pltpu.VMEM((halos, 2, nt, LANES), F32),
            pltpu.VMEM((halos, 2, nt, LANES), F32),
            pltpu.VMEM((halos, 2, SUB, LANES), F32),
            pltpu.VMEM((halos, 2, SUB, LANES), F32),
            pltpu.VMEM((halos, 4, 1, LANES), F32),
            pltpu.VMEM((halos, 4, 1, LANES), F32),
            pltpu.VMEM((halos + 1, total, 1, LANES), F32),
            pltpu.SemaphoreType.DMA((halos, 10)),
            pltpu.SemaphoreType.DMA((halos, 10)),
            pltpu.SemaphoreType.DMA((halos + 1,)),
            pltpu.SemaphoreType.DMA((halos + 1,)),
        ],
        compiler_params=pltpu.CompilerParams(collective_id=0, has_side_effects=True, vmem_limit_bytes=48 * 1024 * 1024),
    )
    results = [call(start[0, 0, 0, p], stencils[:, 0, 0, 0]) for p in range(probes)]
    basis = jnp.stack([r[0] for r in results])
    return basis[None, None, None], jnp.concatenate([r[1] for r in results])


def solution(mesh):
    sizes = tuple(mesh.shape[name] for name in ("gx", "gy", "gz"))
    return jax.shard_map(
        functools.partial(shards, sizes),
        mesh=mesh,
        in_specs=(P("gx", "gy", "gz", None, None, None), P(None, "gx", "gy", "gz", None, None)),
        out_specs=(P("gx", "gy", "gz", None, None, None, None), P()),
        check_vma=False,
    )
```

time: 609 us -> 52.2 us (0.09); the launches traced: 597 us -> 52 us
  blocking collectives: 248 us -> 0 us
  other arithmetic: 92.7 us -> 0 us
  starting transfers between devices: 71.8 us -> 0 us
  local copies, waits for them, and re-layouts: 73 us -> 3.19 us
  matrix products: 51.3 us -> 0 us
  waiting for transfers between devices: 50.3 us -> 0 us
  Pallas kernels: 0 us -> 48.2 us
  between operations: 10.5 us -> 0.65 us
    psum x6 -> x0, blocking collectives: 248 us -> none  [the longest x5 208 us: shards(): lax.psum((jnp.sum(weights[None, None] * stacked * image[None], axis=(2, 3...]
    ppermute x36 -> x0, starting transfers between devices: 71.8 us -> none  [the longest x18 47.2 us: padded_2(): lax.ppermute(lax.slice_in_dim(block, block.shape[dim] - width, None, axis...]
    dot_general x35 -> x0, matrix products: 51.3 us -> none  [along(): jnp.einsum(forms[dim - 1], field, matrix, precision=lax.Precision.HIGHEST)]
    ppermute x36 -> x0, waiting for transfers between devices: 50.3 us -> none  [the longest x18 49.3 us: padded_2(): lax.ppermute(lax.slice_in_dim(block, 0, width, axis=dim), axis, backward)]
    pallas_call x0 -> x1, Pallas kernels: none -> 48.2 us  [shards(): call(start[0, 0, 0, p], stencils[:, 0, 0, 0])]
    slice x42 -> x0, local copies, waits for them, and re-layouts: 27.3 us -> none  [the longest x18 14.4 us: padded_2(): lax.slice_in_dim(block, block.shape[dim] - width, None, axis=dim)]
    unnamed x7 -> x0, other arithmetic: 18.4 us -> none
    another operation x12 -> x0, local copies, waits for them, and re-layouts: 18.1 us -> none
  transfers between devices with their start and end apart: 36 -> 0, of which waited for: 21 -> 0; matrix products, arithmetic and copies ran while one was open for 6% -> 0% of each run, Pallas kernels for 0% -> 0%
where the time goes in v1:
time: 52.2 us; the launch traced here: 52 us
  Pallas kernels  48.2 us (92%)
  local copies, waits for them, and re-layouts  3.19 us (6%)
  between operations  0.65 us (1%)
    pallas_call x1, Pallas kernels, shards(): call(start[0, 0, 0, p], stencils[:, 0, 0, 0])  48.2 us
    unnamed x6, local copies, waits for them, and re-layouts  3.19 us

profile of v1, /device:TPU:0, one launch (start us, length us, event | category | flops | bytes accessed | tf_op | source)
XLA Modules:
  0.0 52.0 jit_solution(13321565403016972971)
XLA Ops:
  0.6 0.0 copy-start
  0.6 0.9 %copy-done = f32[1,1,1,1,32,1024]{5,4,3,2,1,0:T(8,128)S(1)} copy-done((f32[1,1,1,1,32,1024]{5,4,3,2,1,0:T(8,128)S(1)}, f32[1,1,1,1,32,1024]{5,4,3,2,1,0:T(8,128)}, u32[]{:S(2)}) %copy-start) | copy-done | bytes 131096
  1.5 0.0 copy-start.1
  1.5 0.9 %copy-done.1 = f32[6,1,1,1,32,32]{5,4,3,2,1,0:T(8,128)S(1)} copy-done((f32[6,1,1,1,32,32]{5,4,3,2,1,0:T(8,128)S(1)}, f32[6,1,1,1,32,32]{5,4,3,2,1,0:T(8,128)}, u32[]{:S(2)}) %copy-start.1) | copy-done | bytes 24600
  2.4 48.2 %shard_map.41 = (f32[5,32,1024]{2,1,0:T(8,128)S(1)}, f32[1,2,5]{2,1,0:T(2,128)S(1)}) custom-call(f32[32,1024]{1,0:T(8,128)S(1)} %bitcast.4, f32[6,32,32]{2,1,0:T(8,128)S(1)} %bitcast.5), custom_call_target="tpu_custom_call" | custom-call | tf_op jit(solution)/shard_map/pallas_call | solution.py:377
  50.6 0.8 %copy.6 = f32[1,1,1,1,5,32,1024]{6,5,4,3,2,1,0:T(8,128)} copy(f32[1,1,1,1,5,32,1024]{6,5,4,3,2,1,0:T(8,128)S(1)} %bitcast.3) | data formatting | bytes 1310720
  51.5 0.6 %copy.7 = f32[1,2,5]{2,1,0:T(2,128)} copy(f32[1,2,5]{2,1,0:T(2,128)S(1)} %get-tuple-element.9) | data formatting | bytes 80
Async XLA Ops:
  0.6 0.9 %copy-start = (f32[1,1,1,1,32,1024]{5,4,3,2,1,0:T(8,128)S(1)}, f32[1,1,1,1,32,1024]{5,4,3,2,1,0:T(8,128)}, u32[]{:S(2)}) copy-start(f32[1,1,1,1,32,1024]{5,4,3,2,1,0:T(8,128)} %param.2) | copy-start | bytes 393220
  1.5 0.9 %copy-start.1 = (f32[6,1,1,1,32,32]{5,4,3,2,1,0:T(8,128)S(1)}, f32[6,1,1,1,32,32]{5,4,3,2,1,0:T(8,128)}, u32[]{:S(2)}) copy-start(f32[6,1,1,1,32,32]{5,4,3,2,1,0:T(8,128)} %param.3) | copy-start | bytes 73732

commit v2 on v1

--- a/solution.py
+++ b/solution.py
@@ -111,7 +111,7 @@
 
 
 def kernel(sizes, start, st, basis, coef, mx, my, mz, wt, v0, field,
-           zs, zr, xs, xr, ys, yr, es, er, rows, hsend, hrecv, rsend, rrecv):
+           zs, zr, xs, xr, ys, yr, es, er, rows, hsend, hrecv, rsend, rrecv, ready, locals_, images):
     nx, ny, nz = sizes
     total = nx * ny * nz
     count, area = start.shape
@@ -131,11 +131,48 @@
         p = lax.rem(me + k, total)
         return (p // (ny * nz), (p // nz) % ny, p % nz)
 
-    def greet(k, carry):
-        pl.semaphore_signal(barrier, inc=1, device_id=peer(k), device_id_type=MESH)
-        return carry
-
-    lax.fori_loop(1, total, greet, 0)
+    def every_peer(act):
+        if total > 64:
+            def step(k, carry):
+                act(peer(k))
+                return carry
+
+            lax.fori_loop(1, total, step, 0)
+            return
+        around = [[lax.rem(coords[d] + k, sizes[d]) if k else coords[d] for k in range(sizes[d])] for d in range(3)]
+        for ky in range(ny - 1, -1, -1):
+            for kx in range(nx - 1, -1, -1):
+                for kz in range(nz):
+                    if kx or ky or kz:
+                        act((around[0][kx], around[1][ky], around[2][kz]))
+
+    def neighbours(act):
+        for dx in (-1, 0, 1):
+            for dy in (-1, 0, 1):
+                for dz in (-1, 0, 1):
+                    if dx or dy or dz:
+                        target = (px + dx, py + dy, pz + dz)
+                        inside = None
+                        for d, step in enumerate((dx, dy, dz)):
+                            if step:
+                                side = there[d][(step + 1) // 2]
+                                inside = side if inside is None else inside & side
+
+                        @pl.when(inside)
+                        def _():
+                            act(target)
+
+    around_me = 1
+    for d in range(3):
+        around_me = around_me * (1 + (coords[d] > 0).astype(jnp.int32) + (coords[d] < sizes[d] - 1).astype(jnp.int32))
+    around_me = around_me - 1
+
+    rounds = max(sizes) - 2
+
+    def call(r):
+        neighbours(lambda target: pl.semaphore_signal(ready.at[r], inc=1, device_id=target, device_id_type=MESH))
+
+    neighbours(lambda target: pl.semaphore_signal(barrier, inc=1, device_id=target, device_id_type=MESH))
 
     def shared(index, d):
         return ((index == 0) & there[d][0]) | ((index == last) & there[d][1])
@@ -158,67 +195,51 @@
     def tile(t):
         return slice(t * LANES, (t + 1) * LANES)
 
-    def remote(src, dst, phase, slot, target):
-        return pltpu.make_async_remote_copy(
-            src_ref=src, dst_ref=dst, send_sem=hsend.at[phase, slot], recv_sem=hrecv.at[phase, slot],
-            device_id=target, device_id_type=MESH)
-
-    def moved(dx, dy, dz):
-        step = lambda d: 0 if d is None else 2 * d - 1
-        return (px + step(dx), py + step(dy), pz + step(dz))
-
-    def z_copies(phase):
-        return [(remote(zs.at[phase], zr.at[phase, 1 - d], phase, 1 - d, moved(None, None, d)),
-                 there[2][d]) for d in range(2)]
-
-    def xy_copies(phase):
+    def halo_copies(phase):
         out = []
+
+        def add(src, dst, slot, *direction):
+            there_all, target = None, {}
+            for d, step in enumerate(direction):
+                if step is not None:
+                    there_all = there[d][step] if there_all is None else there_all & there[d][step]
+            target = tuple(c if step is None else c + 2 * step - 1 for c, step in zip(coords, direction))
+            copy = pltpu.make_async_remote_copy(
+                src_ref=src, dst_ref=dst.at[phase, slot], send_sem=hsend.at[phase, len(out)],
+                recv_sem=hrecv.at[phase, len(out)], device_id=target, device_id_type=MESH)
+            out.append((copy, there_all, direction, dst, slot))
+
+        for z in (1, 0, None):
+            for d in range(2):
+                for e in range(2):
+                    back = 0 if z is None else 2 - z
+                    add(es.at[phase, 2 * d + e], er, (2 * (1 - d) + 1 - e) * 3 + back, d, e, z)
+        for z in (1, 0, None):
+            back = 0 if z is None else 2 - z
+            for d in range(2):
+                add(xs.at[phase, d], xr, (1 - d) * 3 + back, d, None, z)
+        for z in (1, 0, None):
+            back = 0 if z is None else 2 - z
+            for d in range(2):
+                add(ys.at[phase, d], yr, (1 - d) * 3 + back, None, d, z)
         for d in range(2):
-            out.append((remote(xs.at[phase, d], xr.at[phase, 1 - d], phase, 2 + 1 - d, moved(d, None, None)), there[0][d]))
-            out.append((remote(ys.at[phase, d], yr.at[phase, 1 - d], phase, 4 + 1 - d, moved(None, d, None)), there[1][d]))
-            for e in range(2):
-                slot = 6 + 2 * (1 - d) + 1 - e
-                out.append((remote(es.at[phase, 2 * d + e], er.at[phase, 2 * (1 - d) + 1 - e], phase, slot,
-                                   moved(d, e, None)), there[0][d] & there[1][e]))
+            add(zs.at[phase], zr, 1 - d, None, None, d)
         return out
 
-    def each(copies, act, flip):
-        n = len(copies)
-        for index, (copy, exists) in enumerate(copies):
-            @pl.when(exists)
-            def _():
-                act(copy)
-
-    def send_z(phase):
-        packed = None
-        for t in range(nt):
-            part = jnp.where(face_c, field[:, tile(t)], 0.0)
-            part = part if t == 0 else pltpu.roll(part, 2 * t, 1)
-            packed = part if packed is None else packed + part
-        zs[phase] = packed
-        for copy, exists in z_copies(phase):
+    def start_all(copies):
+        for copy, exists, *_ in copies:
             @pl.when(exists)
             def _():
                 copy.start()
 
-    def wait_slot(ref, slot_sem):
-        pltpu.make_async_copy(ref, ref, slot_sem).wait()
-
-    def finish_halo(phase):
-        for d in range(2):
-            @pl.when(there[2][d])
-            def _():
-                wait_slot(zr.at[phase, d], hrecv.at[phase, d])
-        merged = jnp.where(even, pltpu.roll(zr[phase, 0], LANES - last, 1), pltpu.roll(zr[phase, 1], last, 1))
-        for t in range(nt):
-            part = merged if t == 0 else pltpu.roll(merged, LANES - 2 * t, 1)
-            field[:, tile(t)] += jnp.where(face_c, part, 0.0)
+    def send_halo(phase):
+        copies = halo_copies(phase)
         for d in range(2):
             row = 0 if d == 0 else last
+            for e in range(2):
+                es[phase, 2 * d + e] = field[row:row + 1, tile(0 if e == 0 else nt - 1)]
             for t in range(nt):
                 xs[phase, d, t:t + 1, :] = field[row:row + 1, tile(t)]
-            for e in range(2):
-                es[phase, 2 * d + e] = field[row:row + 1, tile(0 if e == 0 else nt - 1)]
             packed = None
             for i in range(ni):
                 block = field[SUB * i:SUB * (i + 1), tile(0 if d == 0 else nt - 1)]
@@ -227,38 +248,51 @@
                 part = part if shift == 0 else pltpu.roll(part, shift, 1)
                 packed = part if packed is None else packed + part
             ys[phase, d] = packed
-        for copy, exists in xy_copies(phase):
-            @pl.when(exists)
+        packed = None
+        for t in range(nt):
+            part = jnp.where(face_c, field[:, tile(t)], 0.0)
+            part = part if t == 0 else pltpu.roll(part, 2 * t, 1)
+            packed = part if packed is None else packed + part
+        zs[phase] = packed
+        start_all(copies)
+
+    def fold(ref, phase, base):
+        low = ref[phase, base + 1]
+        c = iota(low.shape, 1) & (count - 1)
+        out = ref[phase, base] + jnp.where(c == 0, pltpu.roll(low, LANES - last, 1), 0.0)
+        return out + jnp.where(c == last, pltpu.roll(ref[phase, base + 2], last, 1), 0.0)
+
+    def add_halo(phase):
+        copies = halo_copies(phase)
+        for index, (copy, _, direction, dst, slot) in enumerate(copies):
+            mirror = None
+            for d, step in enumerate(direction):
+                if step is not None:
+                    mirror = there[d][1 - step] if mirror is None else mirror & there[d][1 - step]
+
+            @pl.when(mirror)
             def _():
-                copy.start()
-
-    def add_halo(phase):
+                into = dst.at[phase, slot]
+                pltpu.make_async_copy(into, into, hrecv.at[phase, index]).wait()
+        merged = jnp.where(even, pltpu.roll(zr[phase, 0], LANES - last, 1), pltpu.roll(zr[phase, 1], last, 1))
+        for t in range(nt):
+            part = merged if t == 0 else pltpu.roll(merged, LANES - 2 * t, 1)
+            field[:, tile(t)] += jnp.where(face_c, part, 0.0)
         for d in range(2):
-            @pl.when(there[0][d])
-            def _():
-                wait_slot(xr.at[phase, d], hrecv.at[phase, 2 + d])
-
-            @pl.when(there[1][d])
-            def _():
-                wait_slot(yr.at[phase, d], hrecv.at[phase, 4 + d])
-            for e in range(2):
-                @pl.when(there[0][d] & there[1][e])
-                def _():
-                    wait_slot(er.at[phase, 2 * d + e], hrecv.at[phase, 6 + 2 * d + e])
-        for d in range(2):
-            received = yr[phase, d]
+            received = fold(yr, phase, 3 * d)
             for i in range(ni):
                 shift = (-count * i - d * count) % LANES
                 part = received if shift == 0 else pltpu.roll(received, shift, 1)
                 field[SUB * i:SUB * (i + 1), tile(0 if d == 0 else nt - 1)] += jnp.where(low8 if d == 0 else high8, part, 0.0)
         for d in range(2):
             row = 0 if d == 0 else last
+            received = fold(xr, phase, 3 * d)
             for t in range(nt):
-                line = xr[phase, d, t:t + 1, :]
+                line = received[t:t + 1]
                 if t == 0:
-                    line += jnp.where(lane1 < count, pltpu.roll(er[phase, 2 * d], count, 1), 0.0)
+                    line += jnp.where(lane1 < count, pltpu.roll(fold(er, phase, 6 * d), count, 1), 0.0)
                 if t == nt - 1:
-                    line += jnp.where(lane1 >= LANES - count, pltpu.roll(er[phase, 2 * d + 1], LANES - count, 1), 0.0)
+                    line += jnp.where(lane1 >= LANES - count, pltpu.roll(fold(er, phase, 6 * d + 3), LANES - count, 1), 0.0)
                 field[row:row + 1, tile(t)] += line
 
     def send_dots(phase, products):
@@ -274,13 +308,12 @@
         sums = jnp.sum(packed, axis=1, keepdims=True)
         rows[phase, me] = jnp.sum(jnp.where(diag, sums, 0.0), axis=0, keepdims=True)
 
-        def send(k, carry):
+        def send(target):
             pltpu.make_async_remote_copy(
                 src_ref=rows.at[phase, me], dst_ref=rows.at[phase, me], send_sem=rsend.at[phase],
-                recv_sem=rrecv.at[phase], device_id=peer(k), device_id_type=MESH).start()
-            return carry
-
-        lax.fori_loop(1, total, send, 0)
+                recv_sem=rrecv.at[phase], device_id=target, device_id_type=MESH).start()
+
+        every_peer(send)
 
     def take_dots(phase):
         others = rows.at[phase, pl.ds(0, total - 1)]
@@ -289,40 +322,63 @@
         return jnp.sum(jnp.where(diag, line, 0.0), axis=1, keepdims=True)
 
     build_matrices(st, mx, my, mz)
-    pl.semaphore_wait(barrier, total - 1)
-    send_z(0)
-    finish_halo(0)
+    pl.semaphore_wait(barrier, around_me)
+    send_halo(0)
+    for r in range(rounds):
+        call(r)
+        if r < rounds - 1:
+            pl.semaphore_wait(ready.at[r], around_me)
     add_halo(0)
     vector = field[...]
     alpha = None
     row2, col2 = iota(coef.shape[1:], 0), iota(coef.shape[1:], 1)
     coefs = jnp.zeros(coef.shape[1:], F32)
+    local = apply_patch(vector, mx[...], my[...], mz[...])
+    field[...] = local
+    send_halo(1)
+    if rounds > 0:
+        pl.semaphore_wait(ready.at[rounds - 1], around_me)
+    send_dots(1, [wt[...] * vector * vector, local * vector])
+    add_halo(1)
+    image = field[...]
     for j in range(ITERS):
-        phase = j + 1
-        image = apply_patch(vector, mx[...], my[...], mz[...])
-        field[...] = image
-        send_z(phase)
-        old = [v0[...] if i == 0 else basis[i - 1] for i in range(j)]
-        send_dots(phase, [wt[...] * vector * vector, image * vector] + [image * v for v in old])
-        finish_halo(phase)
-        add_halo(phase)
-        sums = take_dots(phase)
+        more = j < ITERS - 1
+        if more:
+            ahead = apply_patch(image, mx[...], my[...], mz[...])
+            field[...] = ahead
+            send_halo(j + 2)
+        sums = take_dots(j + 1)
         norm = jnp.sqrt(sums[0:1])
         inverse = 1.0 / norm
         if j > 0:
             coefs = jnp.where((row2 == 1) & (col2 == j - 1), norm * alpha, coefs)
         alpha = sums[1:2] / sums[0:1]
         coefs = jnp.where((row2 == 0) & (col2 == j), alpha, coefs)
+        factor = inverse / alpha
+        heights = [sums[2 + i:3 + i] * factor for i in range(j)]
+
+        def follow(applied, unit, old):
+            out = applied * factor - unit
+            for i in range(j):
+                out = out - heights[i] * old(i)
+            return out
+
+        old_vector = lambda i: v0[...] if i == 0 else basis[i - 1]
         unit = vector * inverse
         if j == 0:
             v0[...] = unit
         else:
             basis[j - 1] = unit
-        factor = inverse / alpha
-        following = field[...] * factor - unit
-        for i in range(j):
-            following = following - (sums[2 + i:3 + i] * factor) * old[i]
-        vector = following
+        vector = follow(image, unit, old_vector)
+        if more:
+            unit = local * inverse
+            locals_[j] = unit
+            local = follow(ahead, unit, lambda i: locals_[i])
+            send_dots(j + 2, [wt[...] * vector * vector, local * vector] + [local * old_vector(i) for i in range(j + 1)])
+            unit = image * inverse
+            images[j] = unit
+            add_halo(j + 2)
+            image = follow(field[...], unit, lambda i: images[i])
     send_dots(ITERS + 1, [wt[...] * vector * vector])
     sums = take_dots(ITERS + 1)
     norm = jnp.sqrt(sums[0:1])
@@ -331,7 +387,7 @@
     coef[0] = coefs
 
     for phase in range(ITERS + 1):
-        for copy, exists in z_copies(phase) + xy_copies(phase):
+        for copy, exists, *_ in halo_copies(phase):
             @pl.when(exists)
             def _():
                 copy.wait_send()
@@ -361,16 +417,19 @@
             pltpu.VMEM((halos, count, LANES), F32),
             pltpu.VMEM((halos, 2, count, LANES), F32),
             pltpu.VMEM((halos, 2, nt, LANES), F32),
-            pltpu.VMEM((halos, 2, nt, LANES), F32),
+            pltpu.VMEM((halos, 6, nt, LANES), F32),
             pltpu.VMEM((halos, 2, SUB, LANES), F32),
-            pltpu.VMEM((halos, 2, SUB, LANES), F32),
+            pltpu.VMEM((halos, 6, SUB, LANES), F32),
             pltpu.VMEM((halos, 4, 1, LANES), F32),
-            pltpu.VMEM((halos, 4, 1, LANES), F32),
+            pltpu.VMEM((halos, 12, 1, LANES), F32),
             pltpu.VMEM((halos + 1, total, 1, LANES), F32),
-            pltpu.SemaphoreType.DMA((halos, 10)),
-            pltpu.SemaphoreType.DMA((halos, 10)),
+            pltpu.SemaphoreType.DMA((halos, 26)),
+            pltpu.SemaphoreType.DMA((halos, 26)),
             pltpu.SemaphoreType.DMA((halos + 1,)),
             pltpu.SemaphoreType.DMA((halos + 1,)),
+            pltpu.SemaphoreType.REGULAR((max(1, max(sizes) - 2),)),
+            pltpu.VMEM((ITERS - 1, count, area), F32),
+            pltpu.VMEM((ITERS - 1, count, area), F32),
         ],
         compiler_params=pltpu.CompilerParams(collective_id=0, has_side_effects=True, vmem_limit_bytes=48 * 1024 * 1024),
     )

time: 52.2 us -> 46.2 us (0.89)
  Pallas kernels: 48.2 us -> 42.2 us
    pallas_call x1, Pallas kernels: 48.2 us -> 42.2 us  [shards(): call(start[0, 0, 0, p], stencils[:, 0, 0, 0])]
where the time goes in v2:
time: 46.2 us; the launch traced here: 46 us
  Pallas kernels  42.2 us (91%)
  local copies, waits for them, and re-layouts  3.19 us (7%)
  between operations  0.65 us (1%)
    pallas_call x1, Pallas kernels, shards(): call(start[0, 0, 0, p], stencils[:, 0, 0, 0])  42.2 us
    unnamed x6, local copies, waits for them, and re-layouts  3.19 us

profile of v2, /device:TPU:0, one launch (start us, length us, event | category | flops | bytes accessed | tf_op | source)
XLA Modules:
  0.0 46.0 jit_solution(5688140069459818037)
XLA Ops:
  0.6 0.0 copy-start
  0.6 0.9 %copy-done = f32[1,1,1,1,32,1024]{5,4,3,2,1,0:T(8,128)S(1)} copy-done((f32[1,1,1,1,32,1024]{5,4,3,2,1,0:T(8,128)S(1)}, f32[1,1,1,1,32,1024]{5,4,3,2,1,0:T(8,128)}, u32[]{:S(2)}) %copy-start) | copy-done | bytes 131096
  1.5 0.0 copy-start.1
  1.5 0.9 %copy-done.1 = f32[6,1,1,1,32,32]{5,4,3,2,1,0:T(8,128)S(1)} copy-done((f32[6,1,1,1,32,32]{5,4,3,2,1,0:T(8,128)S(1)}, f32[6,1,1,1,32,32]{5,4,3,2,1,0:T(8,128)}, u32[]{:S(2)}) %copy-start.1) | copy-done | bytes 24600
  2.4 42.2 %shard_map.41 = (f32[5,32,1024]{2,1,0:T(8,128)S(1)}, f32[1,2,5]{2,1,0:T(2,128)S(1)}) custom-call(f32[32,1024]{1,0:T(8,128)S(1)} %bitcast.4, f32[6,32,32]{2,1,0:T(8,128)S(1)} %bitcast.5), custom_call_target="tpu_custom_call" | custom-call | tf_op jit(solution)/shard_map/pallas_call | solution.py:436
  44.6 0.8 %copy.6 = f32[1,1,1,1,5,32,1024]{6,5,4,3,2,1,0:T(8,128)} copy(f32[1,1,1,1,5,32,1024]{6,5,4,3,2,1,0:T(8,128)S(1)} %bitcast.3) | data formatting | bytes 1310720
  45.4 0.6 %copy.7 = f32[1,2,5]{2,1,0:T(2,128)} copy(f32[1,2,5]{2,1,0:T(2,128)S(1)} %get-tuple-element.9) | data formatting | bytes 80
Async XLA Ops:
  0.6 0.9 %copy-start = (f32[1,1,1,1,32,1024]{5,4,3,2,1,0:T(8,128)S(1)}, f32[1,1,1,1,32,1024]{5,4,3,2,1,0:T(8,128)}, u32[]{:S(2)}) copy-start(f32[1,1,1,1,32,1024]{5,4,3,2,1,0:T(8,128)} %param.2) | copy-start | bytes 393220
  1.5 0.9 %copy-start.1 = (f32[6,1,1,1,32,32]{5,4,3,2,1,0:T(8,128)S(1)}, f32[6,1,1,1,32,32]{5,4,3,2,1,0:T(8,128)}, u32[]{:S(2)}) copy-start(f32[6,1,1,1,32,32]{5,4,3,2,1,0:T(8,128)} %param.3) | copy-start | bytes 73732
